TPU v7x, 256 devices: a whole 4x4x8 slice. The times are simulated.
256 devices in a mesh: agent: 128 (over x, y, z), grid: 2 (over core).
Axes of the slice: x: 4, y: 4, z: 8, core: 2. Of those that a mesh axis runs over, the one named last changes fastest.
Arguments:
- value_prior: float32 [2048, 1024], P(None, 'agent'), may hold values from -6 to 6
- trans_weight: float32 [128, 128], replicated, may hold values from 0.05 to 1
- perceived_law_coefficient: float32 [4], replicated, may hold values from 0.7 to 1
- perceived_law_constant: float32 [4], replicated, may hold values from 0.5 to 4
- interest: float32 [4, 16], replicated, may hold values from 0 to 0.05
- wage_level: float32 [4, 16], replicated, may hold values from 0.5 to 1.5
- efficiency: float32 [32], replicated, may hold values from 0.2 to 3
- holdings: float32 [1048576], P('agent'), may hold values from 0 to 40
- shocks: int32 [4, 1048576], P(None, 'agent'), may hold values from 0 to 31
- brackets: int32 [4, 1048576], P(None, 'agent'), may hold values from 0 to 1022
- aggregate: int32 [4], replicated, may hold values from 0 to 3
Outputs:
- value_new: float32 [2048, 1024], P('agent', 'grid')
- policy: float32 [2048, 1024], P('agent', 'grid')
- holdings_final: float32 [1048576], P('agent')
- capital: float32 [4], replicated
All inputs are finite; a program needn't handle non-finite values.
Results may differ from a plain program's by a relative error of at most 0.0003.
Values sent between devices are 32-bit elements; how exact they have to be, the bound alone decides.
A program may use at most 64 MiB of HBM per device.

v0:
```python
import jax
import jax.numpy as jnp
from jax import lax
from jax.sharding import Mesh
from jax.sharding import PartitionSpec as P

A = 1024
E = 32
NK = 16
Z = 4
STATES = 2048
PERIODS = 4
AGENT = ("agent_0", "agent_1", "agent_2")
wealth_upper_limit = 40.0
beta_disc = 0.96
tau_soft = 0.02
floor_cons = 0.1
highest = lax.Precision.HIGHEST


def laid_out(parts, dim):
    parts = jnp.moveaxis(parts, 0, dim)
    shape = parts.shape
    return parts.reshape(*shape[:dim], shape[dim] * shape[dim + 1], *shape[dim + 2 :])


def sent_to_all(x, axis):
    copies = jnp.broadcast_to(x, (lax.axis_size(axis), *x.shape))
    return lax.all_to_all(copies, axis, split_axis=0, concat_axis=0, tiled=True)


def gathered_copies(x, axis, dim):
    return laid_out(sent_to_all(x, axis), dim)


def over_axes(x, axes):
    for axis in axes:
        x = lax.psum(x, axis)
    return x


def make_points():
    fraction = jnp.arange(A, dtype=jnp.float32) / (A - 1)
    return wealth_upper_limit * fraction * fraction


def hat_function_shares(position):
    spacing = wealth_upper_limit / (NK - 1)
    savings_mesh_points = wealth_upper_limit * jnp.arange(NK, dtype=jnp.float32) / (NK - 1)
    return jnp.maximum(0.0, 1.0 - jnp.abs(position[..., None] - savings_mesh_points) / spacing)


def one_hot(indices, number):
    return (indices[:, None] == jnp.arange(number, dtype=jnp.int32)[None, :]).astype(jnp.float32)


def state_parts(states):
    zone_of = states // (NK * E)
    level_of = states // E % NK
    kind_of = states % E
    return (zone_of, level_of, kind_of)


def expect_rows(rows_in, transition, offset_coefficients):
    columns = rows_in.shape[1]
    value_cube = rows_in.reshape(Z, NK, E, columns)
    blended = jnp.einsum(
        "zeyf,ykfn->zekn", transition.reshape(Z, E, Z, E), value_cube, precision=highest
    )
    result = jnp.einsum("zjk,zekn->zjen", offset_coefficients, blended, precision=highest)
    return result.reshape(STATES, columns)


def bellman(points, wealth, expected):
    consume = wealth[:, None] - points[None, :]
    clipped = jnp.maximum(consume, floor_cons)
    utility = jnp.log(clipped) + (consume - clipped) / floor_cons
    scores = (utility + beta_disc * expected[None, :]) / tau_soft
    highest_score = jnp.max(scores, axis=1, keepdims=True)
    weight = jnp.exp(scores - highest_score)
    totals = jnp.sum(weight, axis=1)
    values_now = tau_soft * (highest_score[:, 0] + jnp.log(totals))
    chosen = jnp.sum(weight * points[None, :], axis=1) / totals
    return (values_now, chosen)


def advance(lookup, points, current, shock_row, bracket_row):
    flattened = lookup.reshape(-1)
    flat_index = shock_row * lookup.shape[1] + bracket_row
    value_low = jnp.take(flattened, flat_index)
    value_high = jnp.take(flattened, flat_index + 1)
    edge_low = jnp.take(points, bracket_row)
    edge_high = jnp.take(points, bracket_row + 1)
    fraction = jnp.clip((current - edge_low) / (edge_high - edge_low), 0.0, 1.0)
    return value_low + fraction * (value_high - value_low)


def on_device(
    value_prior,
    trans_weight,
    perceived_law_coefficient,
    perceived_law_constant,
    interest,
    wage_level,
    efficiency,
    holdings,
    shocks,
    brackets,
    aggregate,
):
    agent_count = lax.axis_size(AGENT)
    per_device = STATES // agent_count
    half_rows = A // lax.axis_size("grid")
    first_state = lax.axis_index(AGENT) * per_device
    own_states = first_state + jnp.arange(per_device, dtype=jnp.int32)
    points = make_points()
    transition = trans_weight / jnp.sum(trans_weight, axis=1, keepdims=True)
    savings_mesh_points = wealth_upper_limit * jnp.arange(NK, dtype=jnp.float32) / (NK - 1)
    predicted_stock = jnp.clip(
        perceived_law_coefficient[:, None] * savings_mesh_points[None, :]
        + perceived_law_constant[:, None],
        0.0,
        wealth_upper_limit,
    )
    offset_coefficients = hat_function_shares(predicted_stock)
    partial_value = expect_rows(value_prior, transition, offset_coefficients)
    expected = lax.all_to_all(partial_value, AGENT, split_axis=0, concat_axis=1, tiled=True)
    zone_of, level_of, kind_of = state_parts(own_states)
    price_hot = one_hot(zone_of * NK + level_of, Z * NK)
    interest_own = jnp.sum(price_hot * interest.reshape(1, Z * NK), axis=1)
    wage_own = jnp.sum(price_hot * wage_level.reshape(1, Z * NK), axis=1)
    kind_hot = one_hot(kind_of, E)
    efficiency_own = jnp.sum(kind_hot * efficiency[None, :], axis=1)
    growth = 1.0 + interest_own
    income = wage_own * efficiency_own
    own_points = lax.dynamic_slice_in_dim(points, lax.axis_index("grid") * half_rows, half_rows)

    def one_state(packed):
        column, factor, earned = packed
        return bellman(points, own_points * factor + earned, column)

    values_now, policy = lax.map(one_state, (expected, growth, income))
    agents_total = holdings.shape[0] * agent_count
    halves_in = gathered_copies(policy, "grid", 1)
    policy_cube = lax.all_gather(halves_in, AGENT, axis=0, tiled=True).reshape(Z, NK, E, A)
    current = holdings
    capital_path = []
    for period in range(PERIODS):
        capital = over_axes(jnp.sum(current), AGENT) / agents_total
        capital_path.append(capital)
        knot_weights = hat_function_shares(capital)
        sliced = lax.dynamic_index_in_dim(policy_cube, aggregate[period], 0, keepdims=False)
        lookup = jnp.einsum("k,kea->ea", knot_weights, sliced, precision=highest)
        current = advance(lookup, points, current, shocks[period], brackets[period])
    return (values_now, policy, current, jnp.stack(capital_path))


def solution(mesh):
    finer = Mesh(
        mesh.devices.reshape(4, 4, 8, mesh.shape["grid"]), ("agent_0", "agent_1", "agent_2", "grid")
    )
    in_specs = (
        P(None, AGENT),
        P(),
        P(),
        P(),
        P(),
        P(),
        P(),
        P(AGENT),
        P(None, AGENT),
        P(None, AGENT),
        P(),
    )
    out_specs = (P(AGENT, "grid"), P(AGENT, "grid"), P(AGENT), P())
    return jax.shard_map(
        on_device, mesh=finer, in_specs=in_specs, out_specs=out_specs, check_vma=False
    )
```

profile of v0, /device:TPU:8, one launch (start us, length us, event | category | flops | bytes accessed | tf_op | source)
XLA Modules:
  0.0 961.3 jit_solution(12016140227608750191)
XLA Ops:
  13.5 15.3 %all-to-all-start = ((f32[128,1,128]{2,1,0:T(1,128)}), f32[128,1,128]{2,1,0:T(1,128)S(1)}, u32[]{:S(2)}, u32[]{:S(2)}) async-start(f32[128,1,128]{2,1,0:T(1,128)} %reshape.401), calls=%async_computation | async-start | bytes 131072 | tf_op jit(solution)/shard_map/all_to_all | solution.py:127
  29.6 10.3 %all-to-all-done = f32[128,1,128]{2,1,0:T(1,128)S(1)} async-done(((f32[128,1,128]{2,1,0:T(1,128)}), f32[128,1,128]{2,1,0:T(1,128)S(1)}, u32[]{:S(2)}, u32[]{:S(2)}) %all-to-all-start) | async-done | bytes 65568 | tf_op jit(solution)/shard_map/all_to_all | solution.py:127
  41.7 98.6 %while.14 = (s32[]{:T(128)}, f32[16,512]{1,0:T(8,128)}, f32[16,512]{1,0:T(8,128)S(1)}, f32[16]{0:T(128)S(1)}, f32[512]{0:T(512)S(1)}, /*index=5*/f32[16]{0:T(128)S(1)}, f32[16,1024]{1,0:T(8,128)S(1)}, s32[]{:T(128)}, s32[]{:T(128)}) while((s32[]{:T(128)}, f32[16,512]{1,0:T(8,128)}, f32[16,512]{1,0:T(8,128)S(1)}, ...), condition=%wide.region_8.9_spmd.clone.clone, body=%wide.region_4.8_spmd.clone.clone.sunk | while | flops 9966594 | bytes 63633 | solution.py:142
  51.2 1.4 multiply_reduce_fusion.2
  57.4 1.4 multiply_reduce_fusion.2
  63.6 1.4 multiply_reduce_fusion.2
  69.7 1.4 multiply_reduce_fusion.2
  75.9 1.4 multiply_reduce_fusion.2
  82.1 1.4 multiply_reduce_fusion.2
  88.2 1.4 multiply_reduce_fusion.2
  106.7 1.4 multiply_reduce_fusion.2
  112.9 1.4 multiply_reduce_fusion.2
  140.3 3.8 all_to_all.24
  145.4 9.0 psum.84
  154.4 9.8 %psum.85 = f32[]{:T(128)} all-reduce(f32[]{:T(128)} %psum.84), channel_id=1, replica_groups=mesh['agent_0'=4,'agent_1'=4,'agent_2'=8,'grid'=2] {'agent_1'}, use_global_device_ids=true, to_apply=%region_11.12 | all-reduce | flops 1 | bytes 8 | tf_op jit(solution)/shard_map/psum | solution.py:38
  164.2 15.9 %psum.86 = f32[]{:T(128)} all-reduce(f32[]{:T(128)} %psum.85), channel_id=1, replica_groups=mesh['agent_0'=4,'agent_1'=4,'agent_2'=8,'grid'=2] {'agent_2'}, use_global_device_ids=true, to_apply=%region_12.13 | all-reduce | flops 1 | bytes 8 | tf_op jit(solution)/shard_map/psum | solution.py:38
  186.2 32.9 %gather_fusion.2 = f32[8192]{0:T(1024)S(1)} fusion(f32[1024]{0:T(1024)S(1)} %fusion.55, s32[8192]{0:T(1024)S(1)} %get-tuple-element.165), kind=kCustom, calls=%fused_computation.9.clone | custom fusion | bytes 98304 | tf_op jit(solution)/shard_map/jit(_take)/gather | solution.py:93
  219.1 32.9 %gather_fusion.1 = f32[8192]{0:T(1024)S(1)} fusion(f32[1024]{0:T(1024)S(1)} %fusion.55, s32[8192]{0:T(1024)S(1)} %get-tuple-element.166), kind=kCustom, calls=%fused_computation.1.clone | custom fusion | bytes 98304 | tf_op jit(solution)/shard_map/jit(_take)/gather | solution.py:92
  252.1 32.9 %gather_fusion.6 = f32[8192]{0:T(1024)S(1)} fusion(f32[1024]{0:T(1024)S(1)} %fusion.55, s32[8192]{0:T(1024)S(1)} %get-tuple-element.163), kind=kCustom, calls=%fused_computation.11.clone | custom fusion | bytes 98304 | tf_op jit(solution)/shard_map/jit(_take)/gather | solution.py:93
  284.9 32.9 %gather_fusion.5 = f32[8192]{0:T(1024)S(1)} fusion(f32[1024]{0:T(1024)S(1)} %fusion.55, s32[8192]{0:T(1024)S(1)} %get-tuple-element.164), kind=kCustom, calls=%fused_computation.10.clone | custom fusion | bytes 98304 | tf_op jit(solution)/shard_map/jit(_take)/gather | solution.py:92
  317.9 32.9 %gather_fusion.10 = f32[8192]{0:T(1024)S(1)} fusion(f32[1024]{0:T(1024)S(1)} %fusion.55, s32[8192]{0:T(1024)S(1)} %get-tuple-element.161), kind=kCustom, calls=%fused_computation.13.clone | custom fusion | bytes 98304 | tf_op jit(solution)/shard_map/jit(_take)/gather | solution.py:93
  354.0 6.7 constant_dynamic-slice_fusion.3
  363.0 45.5 %gather_fusion.3 = f32[8192]{0:T(1024)S(1)} fusion(f32[32768]{0:T(1024)S(1)} %bitcast.106, s32[8192]{0:T(1024)S(1)} %get-tuple-element.156), kind=kCustom, calls=%fused_computation.2.clone | custom fusion | bytes 98304 | tf_op jit(solution)/shard_map/jit(_take)/gather | solution.py:91
  408.6 45.5 %gather_fusion = f32[8192]{0:T(1024)S(1)} fusion(f32[32768]{0:T(1024)S(1)} %bitcast.107, s32[8192]{0:T(1024)S(1)} %get-tuple-element.155), kind=kCustom, calls=%fused_computation.clone | custom fusion | bytes 98304 | tf_op jit(solution)/shard_map/jit(_take)/gather | solution.py:90
  454.8 9.4 psum.87
  464.2 32.9 %gather_fusion.9 = f32[8192]{0:T(1024)S(1)} fusion(f32[1024]{0:T(1024)S(1)} %fusion.55, s32[8192]{0:T(1024)S(1)} %get-tuple-element.162), kind=kCustom, calls=%fused_computation.12.clone | custom fusion | bytes 98304 | tf_op jit(solution)/shard_map/jit(_take)/gather | solution.py:92
  497.1 9.5 psum.88
  506.5 4.2 copy.36
  510.7 16.2 %psum.89 = f32[]{:T(128)} all-reduce(f32[]{:T(128)} %psum.88), channel_id=1, replica_groups=mesh['agent_0'=4,'agent_1'=4,'agent_2'=8,'grid'=2] {'agent_2'}, use_global_device_ids=true, to_apply=%region_16.19 | all-reduce | flops 1 | bytes 8 | tf_op jit(solution)/shard_map/psum | solution.py:38
  527.5 2.7 fusion.62
  530.2 45.5 %gather_fusion.7 = f32[8192]{0:T(1024)S(1)} fusion(f32[32768]{0:T(1024)S(1)} %bitcast.108, s32[8192]{0:T(1024)S(1)} %get-tuple-element.154), kind=kCustom, calls=%fused_computation.4.clone | custom fusion | bytes 98304 | tf_op jit(solution)/shard_map/jit(_take)/gather | solution.py:91
  575.8 45.5 %gather_fusion.4 = f32[8192]{0:T(1024)S(1)} fusion(f32[32768]{0:T(1024)S(1)} %bitcast.109, s32[8192]{0:T(1024)S(1)} %get-tuple-element.153), kind=kCustom, calls=%fused_computation.3.clone | custom fusion | bytes 98304 | tf_op jit(solution)/shard_map/jit(_take)/gather | solution.py:90
  622.0 9.2 psum.90
  631.2 32.9 %gather_fusion.14 = f32[8192]{0:T(1024)S(1)} fusion(f32[1024]{0:T(1024)S(1)} %fusion.55, s32[8192]{0:T(1024)S(1)} %get-tuple-element.158), kind=kCustom, calls=%fused_computation.15.clone | custom fusion | bytes 98304 | tf_op jit(solution)/shard_map/jit(_take)/gather | solution.py:93
  664.1 9.0 psum.91
  673.1 4.2 copy.37
  677.2 16.0 %psum.92 = f32[]{:T(128)} all-reduce(f32[]{:T(128)} %psum.91), channel_id=1, replica_groups=mesh['agent_0'=4,'agent_1'=4,'agent_2'=8,'grid'=2] {'agent_2'}, use_global_device_ids=true, to_apply=%region_20.23 | all-reduce | flops 1 | bytes 8 | tf_op jit(solution)/shard_map/psum | solution.py:38
  693.9 2.7 fusion.60
  696.6 45.5 %gather_fusion.11 = f32[8192]{0:T(1024)S(1)} fusion(f32[32768]{0:T(1024)S(1)} %bitcast.110, s32[8192]{0:T(1024)S(1)} %get-tuple-element.152), kind=kCustom, calls=%fused_computation.6.clone | custom fusion | bytes 98304 | tf_op jit(solution)/shard_map/jit(_take)/gather | solution.py:91
  742.1 45.5 %gather_fusion.8 = f32[8192]{0:T(1024)S(1)} fusion(f32[32768]{0:T(1024)S(1)} %bitcast.111, s32[8192]{0:T(1024)S(1)} %get-tuple-element.151), kind=kCustom, calls=%fused_computation.5.clone | custom fusion | bytes 98304 | tf_op jit(solution)/shard_map/jit(_take)/gather | solution.py:90
  788.3 9.4 psum.93
  797.7 32.9 %gather_fusion.13 = f32[8192]{0:T(1024)S(1)} fusion(f32[1024]{0:T(1024)S(1)} %fusion.55, s32[8192]{0:T(1024)S(1)} %get-tuple-element.157), kind=kCustom, calls=%fused_computation.14.clone | custom fusion | bytes 98304 | tf_op jit(solution)/shard_map/jit(_take)/gather | solution.py:92
  830.6 9.5 psum.94
  840.0 2.6 copy.38
  842.6 16.2 %psum.95 = f32[]{:T(128)} all-reduce(f32[]{:T(128)} %psum.94), channel_id=1, replica_groups=mesh['agent_0'=4,'agent_1'=4,'agent_2'=8,'grid'=2] {'agent_2'}, use_global_device_ids=true, to_apply=%region_24.27 | all-reduce | flops 1 | bytes 8 | tf_op jit(solution)/shard_map/psum | solution.py:38
  859.4 2.7 fusion.58
  862.1 45.5 %gather_fusion.15 = f32[8192]{0:T(1024)S(1)} fusion(f32[32768]{0:T(1024)S(1)} %bitcast.112, s32[8192]{0:T(1024)S(1)} %get-tuple-element.159), kind=kCustom, calls=%fused_computation.8.clone | custom fusion | bytes 98304 | tf_op jit(solution)/shard_map/jit(_take)/gather | solution.py:91
  907.7 45.5 %gather_fusion.12 = f32[8192]{0:T(1024)S(1)} fusion(f32[32768]{0:T(1024)S(1)} %bitcast.113, s32[8192]{0:T(1024)S(1)} %get-tuple-element.160), kind=kCustom, calls=%fused_computation.7.clone | custom fusion | bytes 98304 | tf_op jit(solution)/shard_map/jit(_take)/gather | solution.py:90
  (214 shorter events, 102.1 us)
Async XLA Ops:
  10.0 18.9 %copy-start.5 = (f32[4,16]{1,0:T(4,128)S(1)}, f32[4,16]{1,0:T(4,128)}, u32[]{:S(2)}) copy-start(f32[4,16]{1,0:T(4,128)} %param.22) | copy-start | bytes 772
  10.0 19.0 %copy-start.6 = (f32[4,16]{1,0:T(4,128)S(1)}, f32[4,16]{1,0:T(4,128)}, u32[]{:S(2)}) copy-start(f32[4,16]{1,0:T(4,128)} %param.21) | copy-start | bytes 772
  10.1 19.2 %copy-start.7 = (f32[32]{0:T(128)S(1)}, f32[32]{0:T(128)}, u32[]{:S(2)}) copy-start(f32[32]{0:T(128)} %param.23) | copy-start | bytes 388
  13.5 26.4 %all-to-all-start = ((f32[128,1,128]{2,1,0:T(1,128)}), f32[128,1,128]{2,1,0:T(1,128)S(1)}, u32[]{:S(2)}, u32[]{:S(2)}) async-start(f32[128,1,128]{2,1,0:T(1,128)} %reshape.401), calls=%async_computation | async-start | bytes 131072 | tf_op jit(solution)/shard_map/all_to_all | solution.py:127
  28.8 325.1 %all-gather.2.cloned.1.call-start = ((), (), s32[]{:S(2)}) async-start(), calls=%async_computation.2 | async-start | bytes 8454144 | tf_op jit(solution)/shard_map/all_gather | solution.py:145
  41.6 103.1 %copy-start.2 = (f32[8192]{0:T(1024)S(1)}, f32[8192]{0:T(1024)}, u32[]{:S(2)}) copy-start(f32[8192]{0:T(1024)} %param.24) | copy-start | bytes 98308
  41.6 138.5 %copy-start.4 = (s32[4]{0:T(128)S(1)}, s32[4]{0:T(128)}, u32[]{:S(2)}) copy-start(s32[4]{0:T(128)} %param.27) | copy-start | bytes 52
  41.7 144.3 %copy-start = (s32[4,8192]{1,0:T(4,128)S(1)}, s32[4,8192]{1,0:T(4,128)}, u32[]{:S(2)}) copy-start(s32[4,8192]{1,0:T(4,128)} %param.25) | copy-start | bytes 393220
  41.7 144.4 %copy-start.1 = (s32[4,8192]{1,0:T(4,128)S(1)}, s32[4,8192]{1,0:T(4,128)}, u32[]{:S(2)}) copy-start(s32[4,8192]{1,0:T(4,128)} %param.26) | copy-start | bytes 393220
  140.3 78.8 %copy-start.3 = (f32[16,512]{1,0:T(8,128)}, f32[16,512]{1,0:T(8,128)S(1)}, u32[]{:S(2)}) copy-start(f32[16,512]{1,0:T(8,128)S(1)} %get-tuple-element.49) | copy-start | bytes 98308
Sparse Core Ops, SparseCore 0:
  144.9 117.9 all-gather.1
where the time goes:
time: 964 us; the launch traced here: 961 us
  local copies, waits for them, and re-layouts  692 us (72%)
  blocking collectives  143 us (15%)
  other arithmetic  65.1 us (7%)
  between operations  24.8 us (3%)
  starting transfers between devices  15.4 us (2%)
  matrix products  10.4 us (1%)
  waiting for transfers between devices  10.4 us (1%)
    gather x4, local copies, waits for them, and re-layouts, advance(): value_high = jnp.take(flattened, flat_index + 1)  182 us
    gather x4, local copies, waits for them, and re-layouts, advance(): value_low = jnp.take(flattened, flat_index)  182 us
    psum x12, blocking collectives, over_axes(): x = lax.psum(x, axis)  139 us
    gather x4, local copies, waits for them, and re-layouts, advance(): edge_high = jnp.take(points, bracket_row + 1)  131 us
    gather x4, local copies, waits for them, and re-layouts, advance(): edge_low = jnp.take(points, bracket_row)  131 us
    dynamic_update_slice x32, local copies, waits for them, and re-layouts, on_device(): values_now, policy = lax.map(one_state, (expected, growth, income))  22 us
    reduce_sum x16, other arithmetic, bellman(): chosen = jnp.sum(weight * points[None, :], axis=1) / totals  21.9 us
    add x16, other arithmetic, one_state(): return bellman(points, own_points * factor + earned, column)  20.7 us
  transfers between devices with their start and end apart: 2, of which 1 were waited for; matrix products, arithmetic and copies ran while one was open for 17% of the time, Pallas kernels for 0%

commit v1 on v0

--- a/solution.py
+++ b/solution.py
@@ -18,6 +18,12 @@
 highest = lax.Precision.HIGHEST
 
 
+def summed_here(x, name):
+    parts = lax.all_gather(x, name, axis=0, tiled=False)
+    total = parts.sum(axis=0)
+    return total
+
+
 def laid_out(parts, dim):
     parts = jnp.moveaxis(parts, 0, dim)
     shape = parts.shape
@@ -35,7 +41,7 @@
 
 def over_axes(x, axes):
     for axis in axes:
-        x = lax.psum(x, axis)
+        x = summed_here(x, axis)
     return x
 
 

time: 964 us -> 985 us (1.022)
  local copies, waits for them, and re-layouts: 692 us -> 711 us
    psum x12 -> x0, blocking collectives: 139 us -> none  [over_axes(): x = lax.psum(x, axis)]
    unnamed x0 -> x12, blocking collectives: none -> 133 us
    unnamed x23 -> x56, local copies, waits for them, and re-layouts: 13.3 us -> 32.1 us
  transfers between devices with their start and end apart: 2 -> 2, of which waited for: 1 -> 2; matrix products, arithmetic and copies ran while one was open for 17% -> 8% of each run, Pallas kernels for 0% -> 0%
where the time goes in v1:
time: 985 us; the launch traced here: 983 us
  local copies, waits for them, and re-layouts  711 us (72%)
  blocking collectives  137 us (14%)
  other arithmetic  72.3 us (7%)
  between operations  24.7 us (3%)
  starting transfers between devices  15.4 us (2%)
  waiting for transfers between devices  12.2 us (1%)
  matrix products  10.4 us (1%)
    gather x4, local copies, waits for them, and re-layouts, advance(): value_high = jnp.take(flattened, flat_index + 1)  182 us
    gather x4, local copies, waits for them, and re-layouts, advance(): value_low = jnp.take(flattened, flat_index)  182 us
    unnamed x12, blocking collectives  133 us
    gather x4, local copies, waits for them, and re-layouts, advance(): edge_high = jnp.take(points, bracket_row + 1)  131 us
    gather x4, local copies, waits for them, and re-layouts, advance(): edge_low = jnp.take(points, bracket_row)  131 us
    unnamed x56, local copies, waits for them, and re-layouts  32.1 us
    dynamic_update_slice x32, local copies, waits for them, and re-layouts, on_device(): values_now, policy = lax.map(one_state, (expected, growth, income))  22 us
    reduce_sum x16, other arithmetic, bellman(): chosen = jnp.sum(weight * points[None, :], axis=1) / totals  21.9 us
  transfers between devices with their start and end apart: 2, of which 2 were waited for; matrix products, arithmetic and copies ran while one was open for 8% of the time, Pallas kernels for 0%

profile of v1, /device:TPU:8, one launch (start us, length us, event | category | flops | bytes accessed | tf_op | source)
XLA Modules:
  0.0 982.7 jit_solution(15434179907295496186)
XLA Ops:
  13.5 15.3 %all-to-all-start = ((f32[128,1,128]{2,1,0:T(1,128)}), f32[128,1,128]{2,1,0:T(1,128)S(1)}, u32[]{:S(2)}, u32[]{:S(2)}) async-start(f32[128,1,128]{2,1,0:T(1,128)} %reshape.461), calls=%async_computation | async-start | bytes 131072 | tf_op jit(solution)/shard_map/all_to_all | solution.py:133
  29.6 10.3 %all-to-all-done = f32[128,1,128]{2,1,0:T(1,128)S(1)} async-done(((f32[128,1,128]{2,1,0:T(1,128)}), f32[128,1,128]{2,1,0:T(1,128)S(1)}, u32[]{:S(2)}, u32[]{:S(2)}) %all-to-all-start) | async-done | bytes 65568 | tf_op jit(solution)/shard_map/all_to_all | solution.py:133
  41.7 98.6 %while.14 = (s32[]{:T(128)}, f32[16,512]{1,0:T(8,128)}, f32[16,512]{1,0:T(8,128)S(1)}, f32[16]{0:T(128)S(1)}, f32[512]{0:T(512)S(1)}, /*index=5*/f32[16]{0:T(128)S(1)}, f32[16,1024]{1,0:T(8,128)S(1)}, s32[]{:T(128)}, s32[]{:T(128)}) while((s32[]{:T(128)}, f32[16,512]{1,0:T(8,128)}, f32[16,512]{1,0:T(8,128)S(1)}, ...), condition=%wide.region_8.9_spmd.clone.clone, body=%wide.region_4.8_spmd.clone.clone.sunk | while | flops 9966594 | bytes 63633 | solution.py:148
  140.4 3.8 all_to_all.24
  147.4 8.3 all-reduce
  157.0 1.4 dynamic-update-slice.1
  158.4 9.2 all-reduce.1
  168.9 1.4 dynamic-update-slice.2
  170.3 15.3 %all-reduce.2 = f32[8]{0:T(128)S(1)} all-reduce(f32[8]{0:T(128)S(1)} %dynamic-update-slice.2), channel_id=1, replica_groups=mesh['agent_0'=4,'agent_1'=4,'agent_2'=8,'grid'=2] {'agent_2'}, use_global_device_ids=true, to_apply=%add.2 | all-reduce | flops 8 | bytes 64
  191.5 32.9 %gather_fusion.2 = f32[8192]{0:T(1024)S(1)} fusion(f32[1024]{0:T(1024)S(1)} %fusion.55, s32[8192]{0:T(1024)S(1)} %get-tuple-element.165), kind=kCustom, calls=%fused_computation.9.clone | custom fusion | bytes 98304 | tf_op jit(solution)/shard_map/jit(_take)/gather | solution.py:99
  224.4 32.9 %gather_fusion.1 = f32[8192]{0:T(1024)S(1)} fusion(f32[1024]{0:T(1024)S(1)} %fusion.55, s32[8192]{0:T(1024)S(1)} %get-tuple-element.166), kind=kCustom, calls=%fused_computation.1.clone | custom fusion | bytes 98304 | tf_op jit(solution)/shard_map/jit(_take)/gather | solution.py:98
  261.2 1.8 all-gather.2.cloned.1.call-done
  263.0 6.7 constant_dynamic-slice_fusion.3
  272.1 45.5 %gather_fusion.3 = f32[8192]{0:T(1024)S(1)} fusion(f32[32768]{0:T(1024)S(1)} %bitcast.121, s32[8192]{0:T(1024)S(1)} %get-tuple-element.156), kind=kCustom, calls=%fused_computation.2.clone | custom fusion | bytes 98304 | tf_op jit(solution)/shard_map/jit(_take)/gather | solution.py:97
  317.6 45.5 %gather_fusion = f32[8192]{0:T(1024)S(1)} fusion(f32[32768]{0:T(1024)S(1)} %bitcast.122, s32[8192]{0:T(1024)S(1)} %get-tuple-element.155), kind=kCustom, calls=%fused_computation.clone | custom fusion | bytes 98304 | tf_op jit(solution)/shard_map/jit(_take)/gather | solution.py:96
  365.2 32.9 %gather_fusion.6 = f32[8192]{0:T(1024)S(1)} fusion(f32[1024]{0:T(1024)S(1)} %fusion.55, s32[8192]{0:T(1024)S(1)} %get-tuple-element.163), kind=kCustom, calls=%fused_computation.11.clone | custom fusion | bytes 98304 | tf_op jit(solution)/shard_map/jit(_take)/gather | solution.py:99
  398.1 9.2 all-reduce.3
  407.9 1.4 dynamic-update-slice.4
  409.3 32.9 %gather_fusion.5 = f32[8192]{0:T(1024)S(1)} fusion(f32[1024]{0:T(1024)S(1)} %fusion.55, s32[8192]{0:T(1024)S(1)} %get-tuple-element.164), kind=kCustom, calls=%fused_computation.10.clone | custom fusion | bytes 98304 | tf_op jit(solution)/shard_map/jit(_take)/gather | solution.py:98
  442.2 9.5 all-reduce.4
  452.3 1.4 dynamic-update-slice.5
  453.7 4.2 copy.36
  457.9 15.9 %all-reduce.5 = f32[8]{0:T(128)S(1)} all-reduce(f32[8]{0:T(128)S(1)} %dynamic-update-slice.5), channel_id=1, replica_groups=mesh['agent_0'=4,'agent_1'=4,'agent_2'=8,'grid'=2] {'agent_2'}, use_global_device_ids=true, to_apply=%add.5 | all-reduce | flops 8 | bytes 64
  475.0 2.7 fusion.62
  477.7 45.5 %gather_fusion.7 = f32[8192]{0:T(1024)S(1)} fusion(f32[32768]{0:T(1024)S(1)} %bitcast.123, s32[8192]{0:T(1024)S(1)} %get-tuple-element.154), kind=kCustom, calls=%fused_computation.4.clone | custom fusion | bytes 98304 | tf_op jit(solution)/shard_map/jit(_take)/gather | solution.py:97
  523.3 45.5 %gather_fusion.4 = f32[8192]{0:T(1024)S(1)} fusion(f32[32768]{0:T(1024)S(1)} %bitcast.124, s32[8192]{0:T(1024)S(1)} %get-tuple-element.153), kind=kCustom, calls=%fused_computation.3.clone | custom fusion | bytes 98304 | tf_op jit(solution)/shard_map/jit(_take)/gather | solution.py:96
  570.8 32.9 %gather_fusion.10 = f32[8192]{0:T(1024)S(1)} fusion(f32[1024]{0:T(1024)S(1)} %fusion.55, s32[8192]{0:T(1024)S(1)} %get-tuple-element.161), kind=kCustom, calls=%fused_computation.13.clone | custom fusion | bytes 98304 | tf_op jit(solution)/shard_map/jit(_take)/gather | solution.py:99
  603.7 7.7 all-reduce.6
  612.0 1.4 dynamic-update-slice.7
  613.5 32.9 %gather_fusion.9 = f32[8192]{0:T(1024)S(1)} fusion(f32[1024]{0:T(1024)S(1)} %fusion.55, s32[8192]{0:T(1024)S(1)} %get-tuple-element.162), kind=kCustom, calls=%fused_computation.12.clone | custom fusion | bytes 98304 | tf_op jit(solution)/shard_map/jit(_take)/gather | solution.py:98
  646.4 9.8 %all-reduce.7 = f32[4]{0:T(128)S(1)} all-reduce(f32[4]{0:T(128)S(1)} %dynamic-update-slice.7), channel_id=1, replica_groups=mesh['agent_0'=4,'agent_1'=4,'agent_2'=8,'grid'=2] {'agent_1'}, use_global_device_ids=true, to_apply=%add.7 | all-reduce | flops 4 | bytes 32
  656.8 1.5 dynamic-update-slice.8
  658.3 4.2 copy.37
  662.5 14.4 %all-reduce.8 = f32[8]{0:T(128)S(1)} all-reduce(f32[8]{0:T(128)S(1)} %dynamic-update-slice.8), channel_id=1, replica_groups=mesh['agent_0'=4,'agent_1'=4,'agent_2'=8,'grid'=2] {'agent_2'}, use_global_device_ids=true, to_apply=%add.8 | all-reduce | flops 8 | bytes 64
  678.1 2.7 fusion.60
  680.8 45.5 %gather_fusion.11 = f32[8192]{0:T(1024)S(1)} fusion(f32[32768]{0:T(1024)S(1)} %bitcast.125, s32[8192]{0:T(1024)S(1)} %get-tuple-element.152), kind=kCustom, calls=%fused_computation.6.clone | custom fusion | bytes 98304 | tf_op jit(solution)/shard_map/jit(_take)/gather | solution.py:97
  726.3 45.5 %gather_fusion.8 = f32[8192]{0:T(1024)S(1)} fusion(f32[32768]{0:T(1024)S(1)} %bitcast.126, s32[8192]{0:T(1024)S(1)} %get-tuple-element.151), kind=kCustom, calls=%fused_computation.5.clone | custom fusion | bytes 98304 | tf_op jit(solution)/shard_map/jit(_take)/gather | solution.py:96
  773.9 32.9 %gather_fusion.14 = f32[8192]{0:T(1024)S(1)} fusion(f32[1024]{0:T(1024)S(1)} %fusion.55, s32[8192]{0:T(1024)S(1)} %get-tuple-element.158), kind=kCustom, calls=%fused_computation.15.clone | custom fusion | bytes 98304 | tf_op jit(solution)/shard_map/jit(_take)/gather | solution.py:99
  806.8 8.5 all-reduce.9
  815.9 1.4 dynamic-update-slice.10
  817.4 32.9 %gather_fusion.13 = f32[8192]{0:T(1024)S(1)} fusion(f32[1024]{0:T(1024)S(1)} %fusion.55, s32[8192]{0:T(1024)S(1)} %get-tuple-element.157), kind=kCustom, calls=%fused_computation.14.clone | custom fusion | bytes 98304 | tf_op jit(solution)/shard_map/jit(_take)/gather | solution.py:98
  850.2 8.9 all-reduce.10
  859.7 1.4 dynamic-update-slice.11
  861.1 2.6 copy.38
  863.7 15.9 %all-reduce.11 = f32[8]{0:T(128)S(1)} all-reduce(f32[8]{0:T(128)S(1)} %dynamic-update-slice.11), channel_id=1, replica_groups=mesh['agent_0'=4,'agent_1'=4,'agent_2'=8,'grid'=2] {'agent_2'}, use_global_device_ids=true, to_apply=%add.11 | all-reduce | flops 8 | bytes 64
  880.8 2.7 fusion.58
  883.5 45.5 %gather_fusion.15 = f32[8192]{0:T(1024)S(1)} fusion(f32[32768]{0:T(1024)S(1)} %bitcast.127, s32[8192]{0:T(1024)S(1)} %get-tuple-element.159), kind=kCustom, calls=%fused_computation.8.clone | custom fusion | bytes 98304 | tf_op jit(solution)/shard_map/jit(_take)/gather | solution.py:97
  929.1 45.5 %gather_fusion.12 = f32[8192]{0:T(1024)S(1)} fusion(f32[32768]{0:T(1024)S(1)} %bitcast.128, s32[8192]{0:T(1024)S(1)} %get-tuple-element.160), kind=kCustom, calls=%fused_computation.7.clone | custom fusion | bytes 98304 | tf_op jit(solution)/shard_map/jit(_take)/gather | solution.py:96
  (259 shorter events, 129.0 us)
Async XLA Ops:
  10.0 18.9 %copy-start.5 = (f32[4,16]{1,0:T(4,128)S(1)}, f32[4,16]{1,0:T(4,128)}, u32[]{:S(2)}) copy-start(f32[4,16]{1,0:T(4,128)} %param.22) | copy-start | bytes 772
  10.0 19.0 %copy-start.6 = (f32[4,16]{1,0:T(4,128)S(1)}, f32[4,16]{1,0:T(4,128)}, u32[]{:S(2)}) copy-start(f32[4,16]{1,0:T(4,128)} %param.21) | copy-start | bytes 772
  10.1 19.2 %copy-start.7 = (f32[32]{0:T(128)S(1)}, f32[32]{0:T(128)}, u32[]{:S(2)}) copy-start(f32[32]{0:T(128)} %param.23) | copy-start | bytes 388
  13.5 26.4 %all-to-all-start = ((f32[128,1,128]{2,1,0:T(1,128)}), f32[128,1,128]{2,1,0:T(1,128)S(1)}, u32[]{:S(2)}, u32[]{:S(2)}) async-start(f32[128,1,128]{2,1,0:T(1,128)} %reshape.461), calls=%async_computation | async-start | bytes 131072 | tf_op jit(solution)/shard_map/all_to_all | solution.py:133
  28.8 234.2 %all-gather.2.cloned.1.call-start = ((), (), s32[]{:S(2)}) async-start(), calls=%async_computation.2 | async-start | bytes 8454144 | tf_op jit(solution)/shard_map/all_gather | solution.py:151
  41.6 103.2 %copy-start.2 = (f32[8192]{0:T(1024)S(1)}, f32[8192]{0:T(1024)}, u32[]{:S(2)}) copy-start(f32[8192]{0:T(1024)} %param.24) | copy-start | bytes 98308
  41.6 103.8 %copy-start.10 = (u32[256]{0:T(256)S(1)}, u32[256]{0:T(256)}, u32[]{:S(2)}) copy-start(u32[256]{0:T(256)} %constant.175) | copy-start | bytes 3076
  41.7 114.1 %copy-start.9 = (u32[256]{0:T(256)S(1)}, u32[256]{0:T(256)}, u32[]{:S(2)}) copy-start(u32[256]{0:T(256)} %constant.180) | copy-start | bytes 3076
  41.7 126.0 %copy-start.8 = (u32[256]{0:T(256)S(1)}, u32[256]{0:T(256)}, u32[]{:S(2)}) copy-start(u32[256]{0:T(256)} %constant.185) | copy-start | bytes 3076
  41.7 143.9 %copy-start.4 = (s32[4]{0:T(128)S(1)}, s32[4]{0:T(128)}, u32[]{:S(2)}) copy-start(s32[4]{0:T(128)} %param.27) | copy-start | bytes 52
  41.7 149.6 %copy-start = (s32[4,8192]{1,0:T(4,128)S(1)}, s32[4,8192]{1,0:T(4,128)}, u32[]{:S(2)}) copy-start(s32[4,8192]{1,0:T(4,128)} %param.25) | copy-start | bytes 393220
  41.7 149.7 %copy-start.1 = (s32[4,8192]{1,0:T(4,128)S(1)}, s32[4,8192]{1,0:T(4,128)}, u32[]{:S(2)}) copy-start(s32[4,8192]{1,0:T(4,128)} %param.26) | copy-start | bytes 393220
  140.3 84.1 %copy-start.3 = (f32[16,512]{1,0:T(8,128)}, f32[16,512]{1,0:T(8,128)S(1)}, u32[]{:S(2)}) copy-start(f32[16,512]{1,0:T(8,128)S(1)} %get-tuple-element.49) | copy-start | bytes 98308
Sparse Core Ops, SparseCore 0:
  144.9 118.0 all-gather.1
